TPU v7x, 32 devices: a whole 2x2x4 slice. The times are simulated.
32 devices in a mesh: tm: 4 (over z), ent: 2 (over y), batch: 4 (over x, core).
Axes of the slice: x: 2, y: 2, z: 4, core: 2. Of those that a mesh axis runs over, the one named last changes fastest.
Arguments:
- init_state: float32 [4, 1024, 256], P('batch', 'ent'), may hold values from -6 to 6
- tiles: float32 [4, 4, 4, 512, 512], P('batch', 'tm', 'ent'), may hold values from -0.25 to 0.25
- dst_block: int32 [4, 4, 4], P('batch', 'tm', 'ent'), may hold values from 0 to 1
- rel_id: int32 [4, 4, 4], P('batch', 'tm', 'ent'), may hold values from 0 to 255
- cotangent: float32 [4, 4, 1024, 256], P('batch', 'tm', 'ent'), may hold values from -0.125 to 0.125
- rel_emb: float32 [256, 256], replicated, may hold values from -6 to 6
- w_neigh: float32 [256, 256], replicated, may hold values from -0.1875 to 0.1875
- w_self: float32 [256, 256], replicated, may hold values from -0.375 to 0.375
- w_gate: float32 [256, 256], replicated, may hold values from -0.375 to 0.375
- b_gate: float32 [256], replicated, may hold values from -2 to 2
Outputs:
- states: float32 [4, 4, 1024, 256], P('batch', 'tm', 'ent')
- grad_rel: float32 [256, 256], replicated
- grad_neigh: float32 [256, 256], replicated
- grad_self: float32 [256, 256], replicated
- grad_gate: float32 [256, 256], replicated
- grad_bias: float32 [256], replicated
All inputs are finite; a program needn't handle non-finite values.
Results may differ from a plain program's by a relative error of at most 0.00012.
Values sent between devices are 32-bit elements; how exact they have to be, the bound alone decides.
A program may use at most 64 MiB of HBM per device.

v0:
```python
import jax
import jax.numpy as jnp
from jax import lax
from jax.sharding import PartitionSpec as P

highest = lax.Precision.HIGHEST


def shifted(value, axis, steps):
    count = lax.axis_size(axis)
    first, last = (max(0, -steps), min(count, count - steps))
    return lax.ppermute(value, axis, [(source, source + steps) for source in range(first, last)])


def product(left, right):
    return jnp.dot(left, right, precision=highest)


def block_terms(current, tiles_t, rel_t, rel_emb):
    rows_sum = jnp.sum(tiles_t, axis=2)
    rel_pick = (rel_t[:, None] == jnp.arange(rel_emb.shape[0], dtype=jnp.int32)[None, :]).astype(
        jnp.float32
    )
    rel_rows = product(rel_pick, rel_emb)
    result = jnp.einsum("tij,jd->tid", tiles_t, current, precision=highest)
    return result + rows_sum[:, :, None] * rel_rows[:, None, :]


def dest_table(dst_t):
    count = lax.axis_size("ent")
    return (dst_t[:, None] == jnp.arange(count, dtype=jnp.int32)[None, :]).astype(jnp.float32)


def gru_forward(current, incoming, params):
    rel_emb, w_neigh, w_self, w_gate, b_gate = params
    update_gate = jax.nn.sigmoid(product(current, w_gate) + b_gate)
    candidate = jnp.tanh(product(incoming, w_neigh) + product(current, w_self))
    return (update_gate * candidate + (1.0 - update_gate) * current, update_gate, candidate)


def gru_backward(d_new, current, incoming, update_gate, candidate, params):
    rel_emb, w_neigh, w_self, w_gate, b_gate = params
    d_update = d_new * (candidate - current)
    d_cand = d_new * update_gate
    d_pre = d_cand * (1.0 - candidate * candidate)
    d_gate_in = d_update * update_gate * (1.0 - update_gate)
    d_prev = d_new * (1.0 - update_gate) + product(d_pre, w_self.T) + product(d_gate_in, w_gate.T)
    d_incoming = product(d_pre, w_neigh.T)
    dense_grads = (
        product(incoming.T, d_pre),
        product(current.T, d_pre),
        product(current.T, d_gate_in),
        jnp.sum(d_gate_in, axis=0),
    )
    return (d_prev, d_incoming, dense_grads)


def tile_backward(d_res, tiles_t, rel_t, rel_count):
    d_held = jnp.einsum("tij,tid->jd", tiles_t, d_res, precision=highest)
    rows_sum = jnp.sum(tiles_t, axis=2)
    per_tile = jnp.einsum("ti,tid->td", rows_sum, d_res, precision=highest)
    rel_pick = (rel_t[:, None] == jnp.arange(rel_count, dtype=jnp.int32)[None, :]).astype(
        jnp.float32
    )
    return (d_held, jnp.einsum("tr,td->rd", rel_pick, per_tile, precision=highest))


def natural_step(current, tiles_t, dst_t, rel_t, params):
    result = block_terms(current, tiles_t, rel_t, params[0])
    partial_value = jnp.einsum("tg,tid->gid", dest_table(dst_t), result, precision=highest)
    incoming = lax.psum_scatter(partial_value, "ent", scatter_dimension=0, tiled=True)[0]
    return (incoming,) + gru_forward(current, incoming, params)


def natural_spread(d_incoming, dst_t):
    gathered = lax.all_gather(d_incoming[None], "ent", axis=0, tiled=True)
    return jnp.einsum("tg,gid->tid", dest_table(dst_t), gathered, precision=highest)


def run_forward(begin_state, stacks, params, advance_fn):

    def advance(current, inputs):
        tiles_t, dst_t, rel_t = inputs
        incoming, new_state, update_gate, candidate = advance_fn(
            current, tiles_t, dst_t, rel_t, params
        )
        return (new_state, (current, incoming, update_gate, candidate, new_state))

    return lax.scan(advance, begin_state, stacks)


def run_backward(d_last, stored, stacks, targets, params, spread_fn):
    rel_emb = params[0]
    empty = (
        jnp.zeros_like(rel_emb),
        jnp.zeros_like(params[1]),
        jnp.zeros_like(params[2]),
        jnp.zeros_like(params[3]),
        jnp.zeros_like(params[4]),
    )

    def retreat(carry, inputs):
        d_state, weight_sums = carry
        (current, incoming, update_gate, candidate), (tiles_t, dst_t, rel_t), target_t = inputs
        d_new = d_state + target_t
        d_prev, d_incoming, dense_grads = gru_backward(
            d_new, current, incoming, update_gate, candidate, params
        )
        d_res = spread_fn(d_incoming, dst_t)
        d_held, d_rel = tile_backward(d_res, tiles_t, rel_t, rel_emb.shape[0])
        summed = (
            weight_sums[0] + d_rel,
            weight_sums[1] + dense_grads[0],
            weight_sums[2] + dense_grads[1],
            weight_sums[3] + dense_grads[2],
            weight_sums[4] + dense_grads[3],
        )
        return ((d_prev + d_held, summed), None)

    (d_first, weight_sums), unused = lax.scan(
        retreat, (d_last, empty), (stored, stacks, targets), reverse=True
    )
    return (d_first, weight_sums)


def on_device(
    init_state, tiles, dst_block, rel_id, cotangent, rel_emb, w_neigh, w_self, w_gate, b_gate
):
    params = (rel_emb, w_neigh, w_self, w_gate, b_gate)
    n_tm = lax.axis_size("tm")
    stacks = (tiles[0], dst_block[0], rel_id[0])
    targets = cotangent[0]
    is_first = lax.axis_index("tm") == 0
    begin_state = init_state[0]
    stored_all = None
    for round_index in range(n_tm):
        last_state, stored_all = run_forward(begin_state, stacks, params, natural_step)
        if round_index + 1 < n_tm:
            passed = shifted(last_state, "tm", 1)
            begin_state = jnp.where(is_first, init_state[0], passed)
    stored = stored_all[:4]
    d_last = jnp.zeros_like(init_state[0])
    weight_grads = None
    for round_index in range(n_tm):
        d_first, weight_grads = run_backward(
            d_last, stored, stacks, targets, params, natural_spread
        )
        if round_index + 1 < n_tm:
            d_last = shifted(d_first, "tm", -1)
    state_out = stored_all[4][None]
    totals = lax.psum(weight_grads, ("tm", "ent", "batch"))
    return (state_out, totals[0], totals[1], totals[2], totals[3], totals[4])


def solution(mesh):
    placed = (
        P("batch", "ent", None),
        P("batch", "tm", "ent", None, None),
        P("batch", "tm", "ent"),
        P("batch", "tm", "ent"),
        P("batch", "tm", "ent", None),
        P(),
        P(),
        P(),
        P(),
        P(),
    )
    return jax.shard_map(
        on_device,
        mesh=mesh,
        in_specs=placed,
        out_specs=(P("batch", "tm", "ent", None), P(), P(), P(), P(), P()),
        check_vma=False,
    )
```

profile of v0, /device:TPU:0, one launch (start us, length us, event | category | flops | bytes accessed | tf_op | source)
XLA Modules:
  0.0 520.5 jit_solution(6965761714206291700)
XLA Ops:
  7.2 2.0 reduce_sum.32
  9.4 2.9 fusion.12
  12.6 3.5 fusion.66
  18.9 21.7 %reduce-scatter.5.cloned.1.call-done = f32[1,512,256]{2,1,0:T(8,128)} async-done(((f32[2,512,256]{2,1,0:T(8,128)}), f32[1,512,256]{2,1,0:T(8,128)}) %reduce-scatter.5.cloned.1.call-update) | async-done | bytes 524304 | tf_op jit(solution)/shard_map/while/body/eval_jaxpr/reduce_scatter | solution.py:71
  42.2 2.4 fusion.45
  44.7 4.3 collective-permute-start
  49.0 10.4 %collective-permute-done = f32[512,256]{1,0:T(8,128)} collective-permute-done((f32[512,256]{1,0:T(8,128)}, f32[512,256]{1,0:T(8,128)}, u32[]{:S(2)}, u32[]{:S(2)}) %collective-permute-start) | collective-permute-done | bytes 524320 | tf_op jit(solution)/shard_map/ppermute | solution.py:12
  60.2 4.5 fusion.10
  64.8 2.2 copy.28
  67.0 3.8 fusion.63
  71.9 2.4 fusion.42
  74.4 20.1 %reduce-scatter.7.cloned.1.call-done = f32[1,512,256]{2,1,0:T(8,128)} async-done(((f32[2,512,256]{2,1,0:T(8,128)}), f32[1,512,256]{2,1,0:T(8,128)}) %reduce-scatter.7.cloned.1.call-update) | async-done | bytes 524304 | tf_op jit(solution)/shard_map/while/body/eval_jaxpr/reduce_scatter | solution.py:71
  96.1 2.0 fusion.38
  98.1 3.7 collective-permute-start.1
  101.8 10.7 %collective-permute-done.1 = f32[512,256]{1,0:T(8,128)S(1)} collective-permute-done((f32[512,256]{1,0:T(8,128)S(1)}, f32[512,256]{1,0:T(8,128)S(1)}, u32[]{:S(2)}, u32[]{:S(2)}) %collective-permute-start.1) | collective-permute-done | bytes 524320 | tf_op jit(solution)/shard_map/ppermute | solution.py:12
  113.4 4.5 fusion.8
  117.9 2.2 copy.29
  120.2 3.7 fusion.64
  126.5 20.1 %reduce-scatter.9.cloned.1.call-done = f32[1,512,256]{2,1,0:T(8,128)} async-done(((f32[2,512,256]{2,1,0:T(8,128)}), f32[1,512,256]{2,1,0:T(8,128)}) %reduce-scatter.9.cloned.1.call-update) | async-done | bytes 524304 | tf_op jit(solution)/shard_map/while/body/eval_jaxpr/reduce_scatter | solution.py:71
  149.9 3.7 collective-permute-start.2
  153.6 10.7 %collective-permute-done.2 = f32[512,256]{1,0:T(8,128)S(1)} collective-permute-done((f32[512,256]{1,0:T(8,128)S(1)}, f32[512,256]{1,0:T(8,128)S(1)}, u32[]{:S(2)}, u32[]{:S(2)}) %collective-permute-start.2) | collective-permute-done | bytes 524320 | tf_op jit(solution)/shard_map/ppermute | solution.py:12
  164.4 4.5 fusion.6
  168.9 2.2 copy.30
  171.2 3.7 fusion.65
  177.7 19.9 %reduce-scatter.11.cloned.1.call-done = f32[1,512,256]{2,1,0:T(8,128)} async-done(((f32[2,512,256]{2,1,0:T(8,128)}), f32[1,512,256]{2,1,0:T(8,128)}) %reduce-scatter.11.cloned.1.call-update) | async-done | bytes 524304 | tf_op jit(solution)/shard_map/while/body/eval_jaxpr/reduce_scatter | solution.py:71
  197.6 1.7 fusion.73
  199.3 2.7 fusion.145
  204.8 2.5 convolution_add_fusion.1
  207.2 18.5 %all-gather.9.cloned.1.call-done = f32[1024,256]{1,0:T(8,128)} async-done(((f32[512,256]{1,0:T(8,128)}), f32[1024,256]{1,0:T(8,128)}) %all-gather.9.cloned.1.call-update) | async-done | bytes 1048592 | tf_op jit(solution)/shard_map/while/body/eval_jaxpr/all_gather | solution.py:76
  225.7 4.5 fusion.61
  230.2 3.4 fusion.14
  235.8 14.1 %collective-permute-done.3 = f32[512,256]{1,0:T(8,128)S(1)} collective-permute-done((f32[512,256]{1,0:T(8,128)S(1)}, f32[512,256]{1,0:T(8,128)S(1)}, u32[]{:S(2)}, u32[]{:S(2)}) %collective-permute-start.3) | collective-permute-done | bytes 524320 | tf_op jit(solution)/shard_map/ppermute | solution.py:12
  253.2 2.4 fusion.146
  255.6 17.8 %all-gather.11.cloned.1.call-done = f32[1024,256]{1,0:T(8,128)} async-done(((f32[512,256]{1,0:T(8,128)}), f32[1024,256]{1,0:T(8,128)}) %all-gather.11.cloned.1.call-update) | async-done | bytes 1048592 | tf_op jit(solution)/shard_map/while/body/eval_jaxpr/all_gather | solution.py:76
  273.5 4.5 fusion.59
  278.0 3.4 fusion.17
  283.7 14.1 %collective-permute-done.4 = f32[512,256]{1,0:T(8,128)S(1)} collective-permute-done((f32[512,256]{1,0:T(8,128)S(1)}, f32[512,256]{1,0:T(8,128)S(1)}, u32[]{:S(2)}, u32[]{:S(2)}) %collective-permute-start.4) | collective-permute-done | bytes 524320 | tf_op jit(solution)/shard_map/ppermute | solution.py:12
  301.1 2.4 fusion.148
  303.5 17.8 %all-gather.13.cloned.1.call-done = f32[1024,256]{1,0:T(8,128)} async-done(((f32[512,256]{1,0:T(8,128)}), f32[1024,256]{1,0:T(8,128)}) %all-gather.13.cloned.1.call-update) | async-done | bytes 1048592 | tf_op jit(solution)/shard_map/while/body/eval_jaxpr/all_gather | solution.py:76
  321.3 4.5 fusion.57
  325.9 3.4 fusion.20
  331.6 14.1 %collective-permute-done.5 = f32[512,256]{1,0:T(8,128)S(1)} collective-permute-done((f32[512,256]{1,0:T(8,128)S(1)}, f32[512,256]{1,0:T(8,128)S(1)}, u32[]{:S(2)}, u32[]{:S(2)}) %collective-permute-start.5) | collective-permute-done | bytes 524320 | tf_op jit(solution)/shard_map/ppermute | solution.py:12
  348.6 1.7 fusion.151
  350.3 1.7 fusion.152
  353.8 15.1 %all-gather.15.cloned.1.call-done = f32[1024,256]{1,0:T(8,128)} async-done(((f32[512,256]{1,0:T(8,128)}), f32[1024,256]{1,0:T(8,128)}) %all-gather.15.cloned.1.call-update) | async-done | bytes 1048592 | tf_op jit(solution)/shard_map/while/body/eval_jaxpr/all_gather | solution.py:76
  368.8 4.5 fusion.55
  375.1 39.7 %psum.39 = f32[256]{0:T(256)} all-reduce(f32[256]{0:T(256)S(1)} %get-tuple-element.207), channel_id=1, replica_groups=mesh['tm'=4,'ent'=2,'batch'=4] {'tm','ent','batch'}, use_global_device_ids=true, to_apply=%region_10.11 | all-reduce | flops 256 | bytes 2048 | tf_op jit(solution)/shard_map/psum | solution.py:151
  414.8 92.3 %all-reduce.3.cloned.1.call-done = (f32[256,256]{1,0:T(8,128)}, f32[256,256]{1,0:T(8,128)}, f32[256,256]{1,0:T(8,128)}, f32[256,256]{1,0:T(8,128)}) async-done(((f32[256,256]{1,0:T(8,128)}, f32[256,256]{1,0:T(8,128)}, f32[256,256]{1,0:T(8,128)}, f32[256,256]{1,0:T(8,128)}), (f32[256,256]{1,0:T(8,128)}, f32[256,256]{1,0:T(8,128)}, f32[256,256]{1,0:T(8,128)}, ...) | async-done | bytes 1048592 | tf_op jit(solution)/shard_map/psum | solution.py:151
  (142 shorter events, 46.8 us)
Async XLA Ops:
  7.2 35.0 %copy-start = (f32[256,256]{1,0:T(8,128)S(1)}, f32[256,256]{1,0:T(8,128)}, u32[]{:S(2)}) copy-start(f32[256,256]{1,0:T(8,128)} %param.17) | copy-start | bytes 786436
  7.2 2.3 copy-start.1
  7.2 33.4 %reduce-scatter.5.cloned.1.call-start = ((), (), s32[]{:S(2)}) async-start(), calls=%async_computation.4 | async-start | bytes 1572864 | tf_op jit(solution)/shard_map/while/body/eval_jaxpr/reduce_scatter | solution.py:71
  9.2 3.2 copy-start.37
  9.2 3.2 copy-start.42
  9.2 3.4 copy-start.41
  9.4 3.1 copy-start.38
  17.3 23.3 %copy-start.9 = (f32[256,256]{1,0:T(8,128)S(1)}, f32[256,256]{1,0:T(8,128)}, u32[]{:S(2)}) copy-start(f32[256,256]{1,0:T(8,128)} %param.16) | copy-start | bytes 786436
  17.3 77.1 %reduce-scatter.7.cloned.1.call-start = ((), (), s32[]{:S(2)}) async-start(), calls=%async_computation.5 | async-start | bytes 1572864 | tf_op jit(solution)/shard_map/while/body/eval_jaxpr/reduce_scatter | solution.py:71
  44.7 14.7 %collective-permute-start = (f32[512,256]{1,0:T(8,128)}, f32[512,256]{1,0:T(8,128)}, u32[]{:S(2)}, u32[]{:S(2)}) collective-permute-start(f32[512,256]{1,0:T(8,128)} %fusion.45), channel_id=1, source_target_pairs={{0,8},{8,16},{16,24},{1,9},{9,17},{17,25},{2,10},{10,18},{18,26},{... | collective-permute-start | bytes 1572872 | tf_op jit(solution)/shard_map/ppermute | solution.py:12
  71.9 74.7 %reduce-scatter.9.cloned.1.call-start = ((), (), s32[]{:S(2)}) async-start(), calls=%async_computation.6 | async-start | bytes 1572864 | tf_op jit(solution)/shard_map/while/body/eval_jaxpr/reduce_scatter | solution.py:71
  98.1 14.4 %collective-permute-start.1 = (f32[512,256]{1,0:T(8,128)S(1)}, f32[512,256]{1,0:T(8,128)S(1)}, u32[]{:S(2)}, u32[]{:S(2)}) collective-permute-start(f32[512,256]{1,0:T(8,128)S(1)} %fusion.38), channel_id=1, source_target_pairs={{0,8},{8,16},{16,24},{1,9},{9,17},{17,25},{2,10},{10,18},{18,26},{... | collective-permute-start | bytes 1572872 | tf_op jit(solution)/shard_map/ppermute | solution.py:12
  113.4 6.8 %copy-start.39 = (f32[2,512]{0,1:T(8,128)S(1)}, f32[2,512]{0,1:T(8,128)}, u32[]{:S(2)}) copy-start(f32[2,512]{0,1:T(8,128)} %copy-done.38) | copy-start | bytes 12292
  125.0 72.5 %reduce-scatter.11.cloned.1.call-start = ((), (), s32[]{:S(2)}) async-start(), calls=%async_computation.7 | async-start | bytes 1572864 | tf_op jit(solution)/shard_map/while/body/eval_jaxpr/reduce_scatter | solution.py:71
  146.6 17.8 %copy-start.15 = (f32[1,512,256]{2,1,0:T(8,128)S(1)}, f32[1,512,256]{2,1,0:T(8,128)}, u32[]{:S(2)}) copy-start(f32[1,512,256]{2,1,0:T(8,128)} %param.10) | copy-start | bytes 1572868
  149.9 14.4 %collective-permute-start.2 = (f32[512,256]{1,0:T(8,128)S(1)}, f32[512,256]{1,0:T(8,128)S(1)}, u32[]{:S(2)}, u32[]{:S(2)}) collective-permute-start(f32[512,256]{1,0:T(8,128)S(1)} %fusion.31), channel_id=1, source_target_pairs={{0,8},{8,16},{16,24},{1,9},{9,17},{17,25},{2,10},{10,18},{18,26},{... | collective-permute-start | bytes 1572872 | tf_op jit(solution)/shard_map/ppermute | solution.py:12
  164.4 11.7 %copy-start.3 = (f32[512,256]{1,0:T(8,128)}, f32[512,256]{1,0:T(8,128)S(1)}, u32[]{:S(2)}) copy-start(f32[512,256]{1,0:T(8,128)S(1)} %bitcast_select_fusion.2) | copy-start | bytes 1572868
  164.4 6.8 %copy-start.40 = (f32[2,512]{0,1:T(8,128)S(1)}, f32[2,512]{0,1:T(8,128)}, u32[]{:S(2)}) copy-start(f32[2,512]{0,1:T(8,128)} %copy-done.38) | copy-start | bytes 12292
  176.0 49.6 %all-gather.9.cloned.1.call-start = ((), (), s32[]{:S(2)}) async-start(), calls=%async_computation.8 | async-start | bytes 1572864 | tf_op jit(solution)/shard_map/while/body/eval_jaxpr/all_gather | solution.py:76
  177.7 25.1 %copy-start.2 = (f32[1,1,512,256]{3,2,1,0:T(8,128)S(1)}, f32[1,1,512,256]{3,2,1,0:T(8,128)}, u32[]{:S(2)}) copy-start(f32[1,1,512,256]{3,2,1,0:T(8,128)} %param.14) | copy-start | bytes 1572868
  197.6 5.3 %copy-start.10 = (f32[256,256]{1,0:T(8,128)S(1)}, f32[256,256]{1,0:T(8,128)}, u32[]{:S(2)}) copy-start(f32[256,256]{1,0:T(8,128)} %param.16) | copy-start | bytes 786436
  204.2 69.2 %all-gather.11.cloned.1.call-start = ((), (), s32[]{:S(2)}) async-start(), calls=%async_computation.9 | async-start | bytes 1572864 | tf_op jit(solution)/shard_map/while/body/eval_jaxpr/all_gather | solution.py:76
  230.2 3.5 copy-start.16
  230.2 3.5 copy-start.25
  230.2 3.5 copy-start.36
  233.7 16.3 %copy-start.6 = (f32[512,256]{1,0:T(8,128)S(1)}, f32[512,256]{1,0:T(8,128)}, u32[]{:S(2)}) copy-start(f32[512,256]{1,0:T(8,128)} %copy-done.5) | copy-start | bytes 1572868
  234.4 17.1 %copy-start.11 = (f32[256,256]{1,0:T(8,128)S(1)}, f32[256,256]{1,0:T(8,128)}, u32[]{:S(2)}) copy-start(f32[256,256]{1,0:T(8,128)} %param.16) | copy-start | bytes 786436
  234.4 15.5 %collective-permute-start.3 = (f32[512,256]{1,0:T(8,128)S(1)}, f32[512,256]{1,0:T(8,128)S(1)}, u32[]{:S(2)}, u32[]{:S(2)}) collective-permute-start(f32[512,256]{1,0:T(8,128)S(1)} %fusion.23), channel_id=1, source_target_pairs={{8,0},{16,8},{24,16},{9,1},{17,9},{25,17},{10,2},{18,10},{26,18},{... | collective-permute-start | bytes 1572872 | tf_op jit(solution)/shard_map/ppermute | solution.py:12
  253.0 68.4 %all-gather.13.cloned.1.call-start = ((), (), s32[]{:S(2)}) async-start(), calls=%async_computation.10 | async-start | bytes 1572864 | tf_op jit(solution)/shard_map/while/body/eval_jaxpr/all_gather | solution.py:76
  277.9 3.5 copy-start.17
  278.0 3.5 copy-start.26
  278.0 3.5 copy-start.29
  278.0 3.5 copy-start.33
  281.5 16.3 %copy-start.7 = (f32[512,256]{1,0:T(8,128)S(1)}, f32[512,256]{1,0:T(8,128)}, u32[]{:S(2)}) copy-start(f32[512,256]{1,0:T(8,128)} %copy-done.5) | copy-start | bytes 1572868
  282.2 17.1 %copy-start.12 = (f32[256,256]{1,0:T(8,128)S(1)}, f32[256,256]{1,0:T(8,128)}, u32[]{:S(2)}) copy-start(f32[256,256]{1,0:T(8,128)} %param.16) | copy-start | bytes 786436
  282.3 15.5 %collective-permute-start.4 = (f32[512,256]{1,0:T(8,128)S(1)}, f32[512,256]{1,0:T(8,128)S(1)}, u32[]{:S(2)}, u32[]{:S(2)}) collective-permute-start(f32[512,256]{1,0:T(8,128)S(1)} %add_add_fusion.1), channel_id=1, source_target_pairs={{8,0},{16,8},{24,16},{9,1},{17,9},{25,17},{10,2},{18,10},{26,18},{... | collective-permute-start | bytes 1572872 | tf_op jit(solution)/shard_map/ppermute | solution.py:12
  300.8 68.0 %all-gather.15.cloned.1.call-start = ((), (), s32[]{:S(2)}) async-start(), calls=%async_computation.11 | async-start | bytes 1572864 | tf_op jit(solution)/shard_map/while/body/eval_jaxpr/all_gather | solution.py:76
  325.8 3.5 copy-start.18
  325.8 3.5 copy-start.27
  325.8 3.5 copy-start.31
  325.9 3.5 copy-start.34
  329.4 16.3 %copy-start.4 = (f32[512,256]{1,0:T(8,128)S(1)}, f32[512,256]{1,0:T(8,128)}, u32[]{:S(2)}) copy-start(f32[512,256]{1,0:T(8,128)} %copy-done.3) | copy-start | bytes 1572868
  329.4 16.3 %copy-start.8 = (f32[512,256]{1,0:T(8,128)S(1)}, f32[512,256]{1,0:T(8,128)}, u32[]{:S(2)}) copy-start(f32[512,256]{1,0:T(8,128)} %copy-done.5) | copy-start | bytes 1572868
  330.1 16.7 %copy-start.13 = (f32[256,256]{1,0:T(8,128)S(1)}, f32[256,256]{1,0:T(8,128)}, u32[]{:S(2)}) copy-start(f32[256,256]{1,0:T(8,128)} %param.16) | copy-start | bytes 786436
  330.2 15.5 %collective-permute-start.5 = (f32[512,256]{1,0:T(8,128)S(1)}, f32[512,256]{1,0:T(8,128)S(1)}, u32[]{:S(2)}, u32[]{:S(2)}) collective-permute-start(f32[512,256]{1,0:T(8,128)S(1)} %add_add_fusion), channel_id=1, source_target_pairs={{8,0},{16,8},{24,16},{9,1},{17,9},{25,17},{10,2},{18,10},{26,18},{... | collective-permute-start | bytes 1572872 | tf_op jit(solution)/shard_map/ppermute | solution.py:12
  346.9 3.5 copy-start.32
  346.9 5.2 copy-start.35
  348.3 158.7 %all-reduce.3.cloned.1.call-start = ((), (), s32[]{:S(2)}) async-start(), calls=%async_computation.12 | async-start | bytes 2097152 | tf_op jit(solution)/shard_map/psum | solution.py:151
  (11 other events, 10.7 us)
Sparse Core Ops, SparseCore 0:
  17.4 23.1 reduce-scatter.4
  72.0 22.3 reduce-scatter.6
  125.1 21.3 reduce-scatter.8
  176.2 21.3 reduce-scatter.10
  204.4 21.2 all-gather.8
  253.1 20.3 all-gather.10
  300.9 20.3 all-gather.12
  348.4 20.3 all-gather.14
  375.2 131.8 all-reduce.2
where the time goes:
time: 527 us; the launch traced here: 521 us
  waiting for transfers between devices  317 us (60%)
  matrix products  104 us (20%)
  blocking collectives  39.7 us (8%)
  local copies, waits for them, and re-layouts  23.6 us (4%)
  starting transfers between devices  17.4 us (3%)
  between operations  14.8 us (3%)
    psum x1, waiting for transfers between devices, on_device(): totals = lax.psum(weight_grads, ('tm', 'ent', 'batch'))  92.3 us
    reduce_scatter x4, waiting for transfers between devices, natural_step(): lax.psum_scatter(partial_value, 'ent', scatter_dimension=0, tiled=True)[0]  81.7 us
    ppermute x6, waiting for transfers between devices, shifted(): lax.ppermute(value, axis, [(source, source + steps) for source in range(f...  74.1 us
    all_gather x4, waiting for transfers between devices, natural_spread(): gathered = lax.all_gather(d_incoming[None], 'ent', axis=0, tiled=True)  69.2 us
    dot_general x26, matrix products, product(): return jnp.dot(left, right, precision=highest)  42.8 us
    psum x1, blocking collectives, on_device(): totals = lax.psum(weight_grads, ('tm', 'ent', 'batch'))  39.7 us
    dot_general x4, matrix products, natural_spread(): jnp.einsum('tg,gid->tid', dest_table(dst_t), gathered, precision=highest)  17.9 us
    dot_general x4, matrix products, block_terms(): result = jnp.einsum('tij,jd->tid', tiles_t, current, precision=highest)  16.5 us
  transfers between devices with their start and end apart: 15, of which 15 were waited for; matrix products, arithmetic and copies ran while one was open for 4% of the time, Pallas kernels for 0%

commit v1 on v0

--- a/solution.py
+++ b/solution.py
@@ -148,7 +148,7 @@
         if round_index + 1 < n_tm:
             d_last = shifted(d_first, "tm", -1)
     state_out = stored_all[4][None]
-    totals = lax.psum(weight_grads, ("tm", "ent", "batch"))
+    totals = lax.psum(lax.psum(weight_grads, ("ent", "batch")), "tm")
     return (state_out, totals[0], totals[1], totals[2], totals[3], totals[4])
 
 

time: 527 us -> 506 us (0.960)
  blocking collectives: 39.7 us -> 24.5 us
    psum x1 -> x2, blocking collectives: 39.7 us -> 24.5 us  [on_device(): totals = lax.psum(lax.psum(weight_grads, ('ent', 'batch')), 'tm')]
    psum x1 -> x2, waiting for transfers between devices: 92.3 us -> 86.5 us  [on_device(): totals = lax.psum(lax.psum(weight_grads, ('ent', 'batch')), 'tm')]
  transfers between devices with their start and end apart: 15 -> 16, of which waited for: 15 -> 16; matrix products, arithmetic and copies ran while one was open for 4% -> 4% of each run, Pallas kernels for 0% -> 0%
where the time goes in v1:
time: 506 us; the launch traced here: 500 us
  waiting for transfers between devices  312 us (62%)
  matrix products  104 us (21%)
  blocking collectives  24.5 us (5%)
  local copies, waits for them, and re-layouts  23.7 us (5%)
  starting transfers between devices  17.5 us (3%)
  between operations  15.1 us (3%)
    psum x2, waiting for transfers between devices, on_device(): totals = lax.psum(lax.psum(weight_grads, ('ent', 'batch')), 'tm')  86.5 us
    reduce_scatter x4, waiting for transfers between devices, natural_step(): lax.psum_scatter(partial_value, 'ent', scatter_dimension=0, tiled=True)[0]  81.7 us
    ppermute x6, waiting for transfers between devices, shifted(): lax.ppermute(value, axis, [(source, source + steps) for source in range(f...  74.1 us
    all_gather x4, waiting for transfers between devices, natural_spread(): gathered = lax.all_gather(d_incoming[None], 'ent', axis=0, tiled=True)  69.2 us
    dot_general x26, matrix products, product(): return jnp.dot(left, right, precision=highest)  42.6 us
    psum x2, blocking collectives, on_device(): totals = lax.psum(lax.psum(weight_grads, ('ent', 'batch')), 'tm')  24.5 us
    dot_general x4, matrix products, natural_spread(): jnp.einsum('tg,gid->tid', dest_table(dst_t), gathered, precision=highest)  17.9 us
    dot_general x4, matrix products, block_terms(): result = jnp.einsum('tij,jd->tid', tiles_t, current, precision=highest)  16.5 us
  transfers between devices with their start and end apart: 16, of which 16 were waited for; matrix products, arithmetic and copies ran while one was open for 4% of the time, Pallas kernels for 0%

profile of v1, /device:TPU:0, one launch (start us, length us, event | category | flops | bytes accessed | tf_op | source)
XLA Modules:
  0.0 499.9 jit_solution(17315615349145521134)
XLA Ops:
  7.2 2.0 reduce_sum.32
  9.4 2.9 fusion.12
  12.6 3.5 fusion.66
  18.9 21.6 %reduce-scatter.5.cloned.1.call-done = f32[1,512,256]{2,1,0:T(8,128)} async-done(((f32[2,512,256]{2,1,0:T(8,128)}), f32[1,512,256]{2,1,0:T(8,128)}) %reduce-scatter.5.cloned.1.call-update) | async-done | bytes 524304 | tf_op jit(solution)/shard_map/while/body/eval_jaxpr/reduce_scatter | solution.py:71
  42.2 2.4 fusion.45
  44.7 4.4 collective-permute-start
  49.0 10.3 %collective-permute-done = f32[512,256]{1,0:T(8,128)} collective-permute-done((f32[512,256]{1,0:T(8,128)}, f32[512,256]{1,0:T(8,128)}, u32[]{:S(2)}, u32[]{:S(2)}) %collective-permute-start) | collective-permute-done | bytes 524320 | tf_op jit(solution)/shard_map/ppermute | solution.py:12
  60.2 4.5 fusion.10
  64.7 2.3 copy.28
  67.0 3.8 fusion.63
  71.9 2.5 fusion.42
  74.4 20.0 %reduce-scatter.7.cloned.1.call-done = f32[1,512,256]{2,1,0:T(8,128)} async-done(((f32[2,512,256]{2,1,0:T(8,128)}), f32[1,512,256]{2,1,0:T(8,128)}) %reduce-scatter.7.cloned.1.call-update) | async-done | bytes 524304 | tf_op jit(solution)/shard_map/while/body/eval_jaxpr/reduce_scatter | solution.py:71
  96.1 2.0 fusion.38
  98.0 3.7 collective-permute-start.1
  101.7 10.7 %collective-permute-done.1 = f32[512,256]{1,0:T(8,128)S(1)} collective-permute-done((f32[512,256]{1,0:T(8,128)S(1)}, f32[512,256]{1,0:T(8,128)S(1)}, u32[]{:S(2)}, u32[]{:S(2)}) %collective-permute-start.1) | collective-permute-done | bytes 524320 | tf_op jit(solution)/shard_map/ppermute | solution.py:12
  113.3 4.5 fusion.8
  117.8 2.3 copy.29
  120.1 3.7 fusion.64
  126.4 20.1 %reduce-scatter.9.cloned.1.call-done = f32[1,512,256]{2,1,0:T(8,128)} async-done(((f32[2,512,256]{2,1,0:T(8,128)}), f32[1,512,256]{2,1,0:T(8,128)}) %reduce-scatter.9.cloned.1.call-update) | async-done | bytes 524304 | tf_op jit(solution)/shard_map/while/body/eval_jaxpr/reduce_scatter | solution.py:71
  149.8 3.7 collective-permute-start.2
  153.5 10.7 %collective-permute-done.2 = f32[512,256]{1,0:T(8,128)S(1)} collective-permute-done((f32[512,256]{1,0:T(8,128)S(1)}, f32[512,256]{1,0:T(8,128)S(1)}, u32[]{:S(2)}, u32[]{:S(2)}) %collective-permute-start.2) | collective-permute-done | bytes 524320 | tf_op jit(solution)/shard_map/ppermute | solution.py:12
  164.3 4.5 fusion.6
  168.8 2.3 copy.30
  171.1 3.7 fusion.65
  177.6 19.9 %reduce-scatter.11.cloned.1.call-done = f32[1,512,256]{2,1,0:T(8,128)} async-done(((f32[2,512,256]{2,1,0:T(8,128)}), f32[1,512,256]{2,1,0:T(8,128)}) %reduce-scatter.11.cloned.1.call-update) | async-done | bytes 524304 | tf_op jit(solution)/shard_map/while/body/eval_jaxpr/reduce_scatter | solution.py:71
  197.5 1.7 fusion.73
  199.2 2.6 fusion.145
  204.6 2.5 convolution_add_fusion.1
  207.1 18.5 %all-gather.9.cloned.1.call-done = f32[1024,256]{1,0:T(8,128)} async-done(((f32[512,256]{1,0:T(8,128)}), f32[1024,256]{1,0:T(8,128)}) %all-gather.9.cloned.1.call-update) | async-done | bytes 1048592 | tf_op jit(solution)/shard_map/while/body/eval_jaxpr/all_gather | solution.py:76
  225.5 4.5 fusion.61
  230.0 3.4 fusion.14
  235.7 14.1 %collective-permute-done.3 = f32[512,256]{1,0:T(8,128)S(1)} collective-permute-done((f32[512,256]{1,0:T(8,128)S(1)}, f32[512,256]{1,0:T(8,128)S(1)}, u32[]{:S(2)}, u32[]{:S(2)}) %collective-permute-start.3) | collective-permute-done | bytes 524320 | tf_op jit(solution)/shard_map/ppermute | solution.py:12
  253.0 2.4 fusion.146
  255.5 17.9 %all-gather.11.cloned.1.call-done = f32[1024,256]{1,0:T(8,128)} async-done(((f32[512,256]{1,0:T(8,128)}), f32[1024,256]{1,0:T(8,128)}) %all-gather.11.cloned.1.call-update) | async-done | bytes 1048592 | tf_op jit(solution)/shard_map/while/body/eval_jaxpr/all_gather | solution.py:76
  273.3 4.5 fusion.59
  277.9 3.4 fusion.17
  283.6 14.1 %collective-permute-done.4 = f32[512,256]{1,0:T(8,128)S(1)} collective-permute-done((f32[512,256]{1,0:T(8,128)S(1)}, f32[512,256]{1,0:T(8,128)S(1)}, u32[]{:S(2)}, u32[]{:S(2)}) %collective-permute-start.4) | collective-permute-done | bytes 524320 | tf_op jit(solution)/shard_map/ppermute | solution.py:12
  301.0 2.4 fusion.148
  303.4 17.8 %all-gather.13.cloned.1.call-done = f32[1024,256]{1,0:T(8,128)} async-done(((f32[512,256]{1,0:T(8,128)}), f32[1024,256]{1,0:T(8,128)}) %all-gather.13.cloned.1.call-update) | async-done | bytes 1048592 | tf_op jit(solution)/shard_map/while/body/eval_jaxpr/all_gather | solution.py:76
  321.2 4.5 fusion.57
  325.8 3.4 fusion.20
  331.5 14.1 %collective-permute-done.5 = f32[512,256]{1,0:T(8,128)S(1)} collective-permute-done((f32[512,256]{1,0:T(8,128)S(1)}, f32[512,256]{1,0:T(8,128)S(1)}, u32[]{:S(2)}, u32[]{:S(2)}) %collective-permute-start.5) | collective-permute-done | bytes 524320 | tf_op jit(solution)/shard_map/ppermute | solution.py:12
  353.7 15.1 %all-gather.15.cloned.1.call-done = f32[1024,256]{1,0:T(8,128)} async-done(((f32[512,256]{1,0:T(8,128)}), f32[1024,256]{1,0:T(8,128)}) %all-gather.15.cloned.1.call-update) | async-done | bytes 1048592 | tf_op jit(solution)/shard_map/while/body/eval_jaxpr/all_gather | solution.py:76
  368.7 4.5 fusion.55
  375.0 57.1 %all-reduce.5.cloned.1.call-done = (f32[256,256]{1,0:T(8,128)}, f32[256,256]{1,0:T(8,128)}, f32[256,256]{1,0:T(8,128)}, f32[256,256]{1,0:T(8,128)}) async-done(((f32[256,256]{1,0:T(8,128)}, f32[256,256]{1,0:T(8,128)}, f32[256,256]{1,0:T(8,128)}, f32[256,256]{1,0:T(8,128)}), (f32[256,256]{1,0:T(8,128)}, f32[256,256]{1,0:T(8,128)}, f32[256,256]{1,0:T(8,128)}, ...) | async-done | bytes 1048592 | tf_op jit(solution)/shard_map/psum | solution.py:151
  432.1 11.8 %psum.78 = f32[256]{0:T(256)S(1)} all-reduce(f32[256]{0:T(256)S(1)} %get-tuple-element.211), channel_id=1, replica_groups=mesh['tm'=4,'ent'=2,'batch'=4] {'ent','batch'}, use_global_device_ids=true, to_apply=%region_14.15 | all-reduce | flops 256 | bytes 2048 | tf_op jit(solution)/shard_map/psum | solution.py:151
  443.9 12.7 %psum.79 = f32[256]{0:T(256)} all-reduce(f32[256]{0:T(256)S(1)} %psum.78), channel_id=1, replica_groups=mesh['tm'=4,'ent'=2,'batch'=4] {'tm'}, use_global_device_ids=true, to_apply=%region_15.16 | all-reduce | flops 256 | bytes 2048 | tf_op jit(solution)/shard_map/psum | solution.py:151
  456.7 29.5 %all-reduce.7.cloned.1.call-done = (f32[256,256]{1,0:T(8,128)}, f32[256,256]{1,0:T(8,128)}, f32[256,256]{1,0:T(8,128)}, f32[256,256]{1,0:T(8,128)}) async-done(((f32[256,256]{1,0:T(8,128)}, f32[256,256]{1,0:T(8,128)}, f32[256,256]{1,0:T(8,128)}, f32[256,256]{1,0:T(8,128)}), (f32[256,256]{1,0:T(8,128)}, f32[256,256]{1,0:T(8,128)}, f32[256,256]{1,0:T(8,128)}, ...) | async-done | bytes 1048592 | tf_op jit(solution)/shard_map/psum | solution.py:151
  (146 shorter events, 50.3 us)
Async XLA Ops:
  7.2 35.0 %copy-start = (f32[256,256]{1,0:T(8,128)S(1)}, f32[256,256]{1,0:T(8,128)}, u32[]{:S(2)}) copy-start(f32[256,256]{1,0:T(8,128)} %param.17) | copy-start | bytes 786436
  7.2 33.4 %reduce-scatter.5.cloned.1.call-start = ((), (), s32[]{:S(2)}) async-start(), calls=%async_computation.4 | async-start | bytes 1572864 | tf_op jit(solution)/shard_map/while/body/eval_jaxpr/reduce_scatter | solution.py:71
  9.2 3.2 copy-start.37
  9.2 3.2 copy-start.42
  9.2 3.4 copy-start.41
  9.4 3.1 copy-start.38
  17.3 23.3 %copy-start.9 = (f32[256,256]{1,0:T(8,128)S(1)}, f32[256,256]{1,0:T(8,128)}, u32[]{:S(2)}) copy-start(f32[256,256]{1,0:T(8,128)} %param.16) | copy-start | bytes 786436
  17.3 77.1 %reduce-scatter.7.cloned.1.call-start = ((), (), s32[]{:S(2)}) async-start(), calls=%async_computation.5 | async-start | bytes 1572864 | tf_op jit(solution)/shard_map/while/body/eval_jaxpr/reduce_scatter | solution.py:71
  44.7 14.7 %collective-permute-start = (f32[512,256]{1,0:T(8,128)}, f32[512,256]{1,0:T(8,128)}, u32[]{:S(2)}, u32[]{:S(2)}) collective-permute-start(f32[512,256]{1,0:T(8,128)} %fusion.45), channel_id=1, source_target_pairs={{0,8},{8,16},{16,24},{1,9},{9,17},{17,25},{2,10},{10,18},{18,26},{... | collective-permute-start | bytes 1572872 | tf_op jit(solution)/shard_map/ppermute | solution.py:12
  71.9 74.6 %reduce-scatter.9.cloned.1.call-start = ((), (), s32[]{:S(2)}) async-start(), calls=%async_computation.6 | async-start | bytes 1572864 | tf_op jit(solution)/shard_map/while/body/eval_jaxpr/reduce_scatter | solution.py:71
  98.0 14.4 %collective-permute-start.1 = (f32[512,256]{1,0:T(8,128)S(1)}, f32[512,256]{1,0:T(8,128)S(1)}, u32[]{:S(2)}, u32[]{:S(2)}) collective-permute-start(f32[512,256]{1,0:T(8,128)S(1)} %fusion.38), channel_id=1, source_target_pairs={{0,8},{8,16},{16,24},{1,9},{9,17},{17,25},{2,10},{10,18},{18,26},{... | collective-permute-start | bytes 1572872 | tf_op jit(solution)/shard_map/ppermute | solution.py:12
  113.3 6.8 %copy-start.39 = (f32[2,512]{0,1:T(8,128)S(1)}, f32[2,512]{0,1:T(8,128)}, u32[]{:S(2)}) copy-start(f32[2,512]{0,1:T(8,128)} %copy-done.38) | copy-start | bytes 12292
  124.9 72.6 %reduce-scatter.11.cloned.1.call-start = ((), (), s32[]{:S(2)}) async-start(), calls=%async_computation.7 | async-start | bytes 1572864 | tf_op jit(solution)/shard_map/while/body/eval_jaxpr/reduce_scatter | solution.py:71
  146.5 17.8 %copy-start.15 = (f32[1,512,256]{2,1,0:T(8,128)S(1)}, f32[1,512,256]{2,1,0:T(8,128)}, u32[]{:S(2)}) copy-start(f32[1,512,256]{2,1,0:T(8,128)} %param.10) | copy-start | bytes 1572868
  149.8 14.4 %collective-permute-start.2 = (f32[512,256]{1,0:T(8,128)S(1)}, f32[512,256]{1,0:T(8,128)S(1)}, u32[]{:S(2)}, u32[]{:S(2)}) collective-permute-start(f32[512,256]{1,0:T(8,128)S(1)} %fusion.31), channel_id=1, source_target_pairs={{0,8},{8,16},{16,24},{1,9},{9,17},{17,25},{2,10},{10,18},{18,26},{... | collective-permute-start | bytes 1572872 | tf_op jit(solution)/shard_map/ppermute | solution.py:12
  164.3 11.7 %copy-start.3 = (f32[512,256]{1,0:T(8,128)}, f32[512,256]{1,0:T(8,128)S(1)}, u32[]{:S(2)}) copy-start(f32[512,256]{1,0:T(8,128)S(1)} %bitcast_select_fusion.2) | copy-start | bytes 1572868
  164.3 6.8 %copy-start.40 = (f32[2,512]{0,1:T(8,128)S(1)}, f32[2,512]{0,1:T(8,128)}, u32[]{:S(2)}) copy-start(f32[2,512]{0,1:T(8,128)} %copy-done.38) | copy-start | bytes 12292
  175.9 49.6 %all-gather.9.cloned.1.call-start = ((), (), s32[]{:S(2)}) async-start(), calls=%async_computation.8 | async-start | bytes 1572864 | tf_op jit(solution)/shard_map/while/body/eval_jaxpr/all_gather | solution.py:76
  177.5 25.1 %copy-start.2 = (f32[1,1,512,256]{3,2,1,0:T(8,128)S(1)}, f32[1,1,512,256]{3,2,1,0:T(8,128)}, u32[]{:S(2)}) copy-start(f32[1,1,512,256]{3,2,1,0:T(8,128)} %param.14) | copy-start | bytes 1572868
  197.5 5.2 %copy-start.10 = (f32[256,256]{1,0:T(8,128)S(1)}, f32[256,256]{1,0:T(8,128)}, u32[]{:S(2)}) copy-start(f32[256,256]{1,0:T(8,128)} %param.16) | copy-start | bytes 786436
  204.1 69.2 %all-gather.11.cloned.1.call-start = ((), (), s32[]{:S(2)}) async-start(), calls=%async_computation.9 | async-start | bytes 1572864 | tf_op jit(solution)/shard_map/while/body/eval_jaxpr/all_gather | solution.py:76
  230.0 3.5 copy-start.16
  230.0 3.5 copy-start.25
  230.0 3.5 copy-start.36
  233.5 16.2 %copy-start.6 = (f32[512,256]{1,0:T(8,128)S(1)}, f32[512,256]{1,0:T(8,128)}, u32[]{:S(2)}) copy-start(f32[512,256]{1,0:T(8,128)} %copy-done.5) | copy-start | bytes 1572868
  234.2 17.1 %copy-start.11 = (f32[256,256]{1,0:T(8,128)S(1)}, f32[256,256]{1,0:T(8,128)}, u32[]{:S(2)}) copy-start(f32[256,256]{1,0:T(8,128)} %param.16) | copy-start | bytes 786436
  234.2 15.5 %collective-permute-start.3 = (f32[512,256]{1,0:T(8,128)S(1)}, f32[512,256]{1,0:T(8,128)S(1)}, u32[]{:S(2)}, u32[]{:S(2)}) collective-permute-start(f32[512,256]{1,0:T(8,128)S(1)} %fusion.23), channel_id=1, source_target_pairs={{8,0},{16,8},{24,16},{9,1},{17,9},{25,17},{10,2},{18,10},{26,18},{... | collective-permute-start | bytes 1572872 | tf_op jit(solution)/shard_map/ppermute | solution.py:12
  252.8 68.4 %all-gather.13.cloned.1.call-start = ((), (), s32[]{:S(2)}) async-start(), calls=%async_computation.10 | async-start | bytes 1572864 | tf_op jit(solution)/shard_map/while/body/eval_jaxpr/all_gather | solution.py:76
  277.8 3.5 copy-start.17
  277.8 3.5 copy-start.26
  277.8 3.5 copy-start.29
  277.8 3.5 copy-start.33
  281.4 16.3 %copy-start.7 = (f32[512,256]{1,0:T(8,128)S(1)}, f32[512,256]{1,0:T(8,128)}, u32[]{:S(2)}) copy-start(f32[512,256]{1,0:T(8,128)} %copy-done.5) | copy-start | bytes 1572868
  282.1 17.2 %copy-start.12 = (f32[256,256]{1,0:T(8,128)S(1)}, f32[256,256]{1,0:T(8,128)}, u32[]{:S(2)}) copy-start(f32[256,256]{1,0:T(8,128)} %param.16) | copy-start | bytes 786436
  282.1 15.5 %collective-permute-start.4 = (f32[512,256]{1,0:T(8,128)S(1)}, f32[512,256]{1,0:T(8,128)S(1)}, u32[]{:S(2)}, u32[]{:S(2)}) collective-permute-start(f32[512,256]{1,0:T(8,128)S(1)} %add_add_fusion.1), channel_id=1, source_target_pairs={{8,0},{16,8},{24,16},{9,1},{17,9},{25,17},{10,2},{18,10},{26,18},{... | collective-permute-start | bytes 1572872 | tf_op jit(solution)/shard_map/ppermute | solution.py:12
  300.7 68.0 %all-gather.15.cloned.1.call-start = ((), (), s32[]{:S(2)}) async-start(), calls=%async_computation.11 | async-start | bytes 1572864 | tf_op jit(solution)/shard_map/while/body/eval_jaxpr/all_gather | solution.py:76
  325.7 3.5 copy-start.18
  325.7 3.5 copy-start.27
  325.7 3.5 copy-start.31
  325.7 3.5 copy-start.34
  329.2 16.3 %copy-start.4 = (f32[512,256]{1,0:T(8,128)S(1)}, f32[512,256]{1,0:T(8,128)}, u32[]{:S(2)}) copy-start(f32[512,256]{1,0:T(8,128)} %copy-done.3) | copy-start | bytes 1572868
  329.3 16.3 %copy-start.8 = (f32[512,256]{1,0:T(8,128)S(1)}, f32[512,256]{1,0:T(8,128)}, u32[]{:S(2)}) copy-start(f32[512,256]{1,0:T(8,128)} %copy-done.5) | copy-start | bytes 1572868
  330.0 16.7 %copy-start.13 = (f32[256,256]{1,0:T(8,128)S(1)}, f32[256,256]{1,0:T(8,128)}, u32[]{:S(2)}) copy-start(f32[256,256]{1,0:T(8,128)} %param.16) | copy-start | bytes 786436
  330.0 15.5 %collective-permute-start.5 = (f32[512,256]{1,0:T(8,128)S(1)}, f32[512,256]{1,0:T(8,128)S(1)}, u32[]{:S(2)}, u32[]{:S(2)}) collective-permute-start(f32[512,256]{1,0:T(8,128)S(1)} %add_add_fusion), channel_id=1, source_target_pairs={{8,0},{16,8},{24,16},{9,1},{17,9},{25,17},{10,2},{18,10},{26,18},{... | collective-permute-start | bytes 1572872 | tf_op jit(solution)/shard_map/ppermute | solution.py:12
  346.8 3.5 copy-start.32
  346.8 5.2 %copy-start.35 = (f32[1,512,256]{2,1,0:T(8,128)S(1)}, f32[1,512,256]{2,1,0:T(8,128)}, u32[]{:S(2)}) copy-start(f32[1,512,256]{2,1,0:T(8,128)} %reduce-scatter.11.cloned.1.call-done) | copy-start | bytes 1572868
  348.2 83.9 %all-reduce.5.cloned.1.call-start = ((), (), s32[]{:S(2)}) async-start(), calls=%async_computation.12 | async-start | bytes 2097152 | tf_op jit(solution)/shard_map/psum | solution.py:151
  375.0 111.1 %all-reduce.7.cloned.1.call-start = ((), (), s32[]{:S(2)}) async-start(), calls=%async_computation.13 | async-start | bytes 2097152 | tf_op jit(solution)/shard_map/psum | solution.py:151
  (12 other events, 13.0 us)
Sparse Core Ops, SparseCore 0:
  17.4 23.1 reduce-scatter.4
  72.0 22.3 reduce-scatter.6
  125.0 21.3 reduce-scatter.8
  176.0 21.3 reduce-scatter.10
  204.2 21.2 all-gather.8
  252.9 20.3 all-gather.10
  300.8 20.3 all-gather.12
  348.3 20.3 all-gather.14
  375.1 56.9 all-reduce.4
  434.5 51.5 all-reduce.6
